TPU v7x, 32 devices: a whole 2x2x4 slice. The times are simulated.
32 devices in a mesh: sub: 16 (over z, y, core), tm: 2 (over x).
Axes of the slice: x: 2, y: 2, z: 4, core: 2. Of those that a mesh axis runs over, the one named last changes fastest.
Arguments:
- voltages: bfloat16 [192, 2, 96, 2048], P('sub', None, None, 'tm'), may hold values from -6 to 6
- pointing_table: bfloat16 [192, 2, 320, 96], P('sub'), may hold values from -0.4375 to 0.4375
- beam_pointing: int32 [256], replicated, may hold values from 0 to 319
- subband_order: int32 [192], replicated, may hold values from 0 to 191, each once
- live_subbands: int32 [1], replicated, may hold values from 152 to 192
- filter_taps: float32 [16, 16], replicated, may hold values from -0.36 to 0.36
Outputs:
- synthesised: bfloat16 [256, 12, 2, 32768], P('sub', None, None, 'tm')
Inputs may be any that keep to these rules, and one draw needn't show every extreme that they name: `subband_order`: each slot is named by exactly one frequency.
All inputs are finite; a program needn't handle non-finite values.
Results may differ from a plain program's by a relative error of at most 0.0052.
Values may be sent and summed in bfloat16 or wider, within the bound.
A program may use at most 192 MiB of HBM per device.

v0:
```python
import functools
import math

import jax
import jax.numpy as jnp
from jax import lax
from jax.experimental import pallas as pl
from jax.experimental.pallas import tpu as pltpu
from jax.sharding import PartitionSpec as P

LANES = 128
VMEM = 60 * 1024 * 1024


def inverse_table(channel_count):
    channel_index = jnp.arange(channel_count, dtype=jnp.int32)
    phase = (jnp.outer(channel_index, channel_index) % channel_count).astype(jnp.float32) * (
        2.0 * math.pi / channel_count
    )
    cosine = jnp.cos(phase).astype(jnp.bfloat16)
    sine_table = jnp.sin(phase).astype(jnp.bfloat16)
    upper_rows = jnp.stack([cosine, -sine_table], axis=1)
    lower_rows = jnp.stack([sine_table, cosine], axis=1)
    return jnp.stack([upper_rows, lower_rows], axis=0)


def synthesis_matrix(filter_taps, inner, reach):
    tap_count, chan = filter_taps.shape
    table = inverse_table(chan).astype(jnp.float32)
    delta = jnp.arange(reach)[:, None, None]
    tl_in = jnp.arange(inner)[None, :, None]
    tl_out = jnp.arange(inner)[None, None, :]
    tap = inner * delta + tl_out - tl_in
    inside = (tap >= 0) & (tap < tap_count)
    taps = jnp.where(inside[..., None], filter_taps[jnp.clip(tap, 0, tap_count - 1)], 0.0)
    full = (
        taps[:, None, :, None, None, :, :]
        * table.transpose(2, 3, 0, 1)[None, :, None, :, :, None, :]
    )
    return full.reshape(reach * 2 * inner * chan, 2 * inner * chan).astype(jnp.bfloat16)


def form_kernel(inner, groups, with_rim, hot_ref, perm_ref, table_ref, volt_ref, *rest):
    chunks = rest[-len(groups) :]
    f32, bf16 = jnp.float32, jnp.bfloat16
    real, imag = table_ref[0, 0], table_ref[0, 1]
    both = jnp.concatenate(
        [
            jnp.concatenate([real, -imag], axis=1),
            jnp.concatenate([imag, real], axis=1),
        ],
        axis=0,
    )
    weights = jnp.dot(hot_ref[...], both, preferred_element_type=f32).astype(bf16)
    if with_rim:
        rim_ref, rim_out = rest[0], rest[1]
        rim_out[0] = jnp.dot(weights, rim_ref[0], preferred_element_type=f32).astype(bf16)
    signal = jnp.dot(volt_ref[0], perm_ref[...], preferred_element_type=f32).astype(bf16)
    start = 0 if with_rim else hot_ref.shape[0] - 2 * sum(groups) * chunks[0].shape[0]
    for group, out in zip(groups, chunks):
        rows = 2 * group * out.shape[0]
        formed = jnp.dot(
            weights[start : start + rows], signal, preferred_element_type=f32
        ).astype(bf16)
        start += rows
        for d in range(out.shape[0]):
            for tl in range(inner):
                out[d, 0, tl] = formed[
                    2 * d * group : 2 * (d + 1) * group, tl * LANES : (tl + 1) * LANES
                ]


def synth_kernel(
    inner, chan, group, reach, local, order_ref, live_ref, z_ref, rim_ref, mat_ref, *rest
):
    out_ref, held, wide, line, stacked, made, sems = rest[-7:]
    g = pl.program_id(0)
    count = pl.num_programs(0)
    f32, bf16 = jnp.float32, jnp.bfloat16

    def fetch(step, slot):
        named = [order_ref[step * chan + c] for c in range(chan)]
        return [
            pltpu.make_async_copy(
                z_ref.at[lax.div(at, local), pl.ds(lax.rem(at, local) * inner, inner)],
                held.at[slot, c],
                sems.at[slot],
            )
            for c, at in enumerate(named)
        ]

    slot = lax.rem(g, 2)

    @pl.when(g == 0)
    def _():
        for copy in fetch(0, 0):
            copy.start()

    @pl.when(g + 1 < count)
    def _():
        for copy in fetch(g + 1, 1 - slot):
            copy.start()

    for copy in fetch(g, slot):
        copy.wait()

    pair = 2 * group
    for c in range(chan):
        alive = g * chan + c < live_ref[0]
        for tl in range(inner):
            block = held[slot, c, tl].astype(f32)
            wide[tl, c * pair : (c + 1) * pair, :] = jnp.where(alive, block, 0.0)

    width = inner * chan

    def turn(b, carry):
        base = pl.multiple_of(b * LANES, LANES)
        for p in range(2):
            rows = [
                wide[tl, pl.ds(p * group + b, chan, stride=pair), :] for tl in range(inner)
            ]
            line[p, 8 : 8 + LANES, :] = jnp.concatenate(rows, axis=0).T
            line[p, 8 - (reach - 1) : 8, :] = rim_ref[0, b, p]
            for delta in range(reach):
                at = (2 * delta + p) * width
                stacked[pl.ds(base, LANES), at : at + width] = line[
                    p, 8 - delta : 8 - delta + LANES, :
                ].astype(bf16)
        return carry

    lax.fori_loop(0, group, turn, 0, unroll=2)

    def emit(b, carry):
        base = pl.multiple_of(b * 2 * LANES, 2 * LANES)
        out = jnp.dot(
            stacked[pl.ds(base, 2 * LANES), :], mat_ref[...], preferred_element_type=f32
        )
        for i in range(2):
            for q in range(2):
                made[i, q * LANES : (q + 1) * LANES, :] = out[
                    i * LANES : (i + 1) * LANES, q * width : (q + 1) * width
                ]
        for i in range(2):
            for tb in range(LANES):
                both = made[i, pl.ds(tb, 2, stride=LANES), :].astype(bf16)
                out_ref[2 * b + i, 0, :, tb * LANES : (tb + 1) * LANES] = both
        return carry

    lax.fori_loop(0, group // 2, emit, 0)


def on_device(voltages, pointing_table, beam_pointing, subband_order, live_subbands, filter_taps):
    local_subbands, _, inputs, local_time = voltages.shape
    pointings = pointing_table.shape[2]
    beam_count = beam_pointing.shape[0]
    slots = subband_order.shape[0]
    tap_count, chan = filter_taps.shape
    inner = LANES // chan
    assert local_time == inner * LANES
    reach = 1 + -(-(tap_count - 1) // inner)
    rim_len = (reach - 1) * inner
    devices = lax.axis_size("sub")
    beam_part = beam_count // devices
    quarter = beam_part // 4
    if beam_part % 8 == 0:
        groups, firsts = [quarter, 2 * quarter, quarter], [0, 2 * quarter, quarter]
    else:
        groups, firsts = [beam_part], [0]
    starts = [sum(groups[:h]) for h in range(len(groups))]
    bands = slots // chan

    signal = voltages.reshape(local_subbands, 2 * inputs, local_time)
    times = range(lax.axis_size("tm"))
    route = [(i - 1, i) for i in times if i > 0]
    rim = lax.ppermute(signal[:, :, local_time - rim_len :], "tm", route)
    rim = jnp.pad(rim, ((0, 0), (0, 0), (0, LANES - rim_len)))

    picks = beam_pointing.reshape(devices, beam_part)
    wanted = jnp.concatenate(
        [
            (
                picks[:, None, first : first + group]
                + pointings * jnp.arange(2, dtype=jnp.int32)[:, None]
            ).reshape(-1)
            for first, group in zip(firsts, groups)
        ]
    )
    hot = (wanted[:, None] == jnp.arange(2 * pointings)[None, :]).astype(jnp.bfloat16)
    source = jnp.arange(local_time, dtype=jnp.int32)
    place = (source % inner) * LANES + source // inner
    perm = (place[:, None] == source[None, :]).astype(jnp.bfloat16)

    def form(groups, signal, rim):
        with_rim = rim is not None
        pieces = [(devices, local_subbands, inner, 2 * group, LANES) for group in groups]
        rim_size = (local_subbands, hot.shape[0], LANES)
        return pl.pallas_call(
            functools.partial(form_kernel, inner, groups, with_rim),
            grid=(local_subbands,),
            in_specs=[
                pl.BlockSpec(hot.shape, lambda s: (0, 0)),
                pl.BlockSpec(perm.shape, lambda s: (0, 0)),
                pl.BlockSpec((1, 2, pointings, inputs), lambda s: (s, 0, 0, 0)),
                pl.BlockSpec((1, 2 * inputs, local_time), lambda s: (s, 0, 0)),
            ]
            + [pl.BlockSpec((1, 2 * inputs, LANES), lambda s: (s, 0, 0))] * with_rim,
            out_specs=[pl.BlockSpec((1,) + rim_size[1:], lambda s: (s, 0, 0))] * with_rim
            + [
                pl.BlockSpec((size[0], 1) + size[2:], lambda s: (0, s, 0, 0, 0))
                for size in pieces
            ],
            out_shape=[jax.ShapeDtypeStruct(rim_size, jnp.bfloat16)] * with_rim
            + [jax.ShapeDtypeStruct(size, jnp.bfloat16) for size in pieces],
            compiler_params=pltpu.CompilerParams(vmem_limit_bytes=VMEM),
            cost_estimate=pl.CostEstimate(
                flops=12_000_000_000, bytes_accessed=20_000_000, transcendentals=0
            ),
            name="form",
        )(hot, perm, pointing_table, signal, *([rim] if with_rim else []))

    edge, opening = form(groups[:1], signal, rim)
    pieces = [opening]
    if len(groups) > 1:
        later, _ = lax.optimization_barrier((signal, opening))
        pieces += form(groups[1:], later, None)

    mat = synthesis_matrix(filter_taps, inner, reach)

    edge = edge[:, :, :rim_len]
    edge = jnp.concatenate(
        [
            edge[:, 2 * devices * start : 2 * devices * (start + group)].reshape(
                local_subbands, devices, 2 * group * rim_len
            )
            for start, group in zip(starts, groups)
        ],
        axis=2,
    )
    edge = edge.swapaxes(0, 1).reshape(devices, -1)
    edge_size = edge.shape[1]
    planes = -(-edge_size // (2 * groups[0] * LANES))
    edge = jnp.pad(edge, ((0, 0), (0, planes * 2 * groups[0] * LANES - edge_size)))
    edge = edge.reshape(devices, planes, 2 * groups[0], LANES)
    pieces = [
        piece.reshape(devices, local_subbands * inner, 2 * group, LANES)
        for piece, group in zip(pieces, groups)
    ]
    pieces[0] = jnp.concatenate([pieces[0], edge], axis=1)
    got = [lax.all_to_all(p, "sub", split_axis=0, concat_axis=0, tiled=True) for p in pieces]
    edge = got[0][:, local_subbands * inner :].reshape(devices, -1)[:, :edge_size]
    edge = jnp.take(edge.reshape(slots, -1), subband_order, axis=0)
    live_mask = jnp.arange(slots, dtype=jnp.int32) < live_subbands[0]
    edge = jnp.where(live_mask[:, None], edge.astype(jnp.float32), 0.0)

    def edge_of(start, group):
        part = edge[:, 2 * start * rim_len : 2 * (start + group) * rim_len]
        part = part.reshape(bands, chan, 2, group, reach - 1, inner)
        return part.transpose(0, 3, 2, 4, 5, 1).reshape(
            bands, group, 2, reach - 1, inner * chan
        )

    result = None
    for first, start, group, z in zip(firsts, starts, groups, got):
        operands = [subband_order, live_subbands, z, edge_of(start, group), mat]
        in_specs = [
            pl.BlockSpec(memory_space=pl.ANY),
            pl.BlockSpec((1, group, 2, reach - 1, LANES), lambda g, *_: (g, 0, 0, 0, 0)),
            pl.BlockSpec(mat.shape, lambda g, *_: (0, 0)),
        ]
        alias = {}
        if result is not None:
            operands.append(result)
            in_specs.append(pl.BlockSpec(memory_space=pl.ANY))
            alias = {5: 0}
        result = pl.pallas_call(
            functools.partial(synth_kernel, inner, chan, group, reach, local_subbands),
            grid_spec=pltpu.PrefetchScalarGridSpec(
                num_scalar_prefetch=2,
                grid=(bands,),
                in_specs=in_specs,
                out_specs=pl.BlockSpec(
                    (group, 1, 2, local_time * chan), functools.partial(lambda h, g, *_: (h, g, 0, 0), first // group)
                ),
                scratch_shapes=[
                    pltpu.VMEM((2, chan, inner, 2 * group, LANES), jnp.bfloat16),
                    pltpu.VMEM((inner, chan * 2 * group, LANES), jnp.float32),
                    pltpu.VMEM((2, 8 + LANES, LANES), jnp.float32),
                    pltpu.VMEM((group * LANES, mat.shape[0]), jnp.bfloat16),
                    pltpu.VMEM((2, 2 * LANES, LANES), jnp.float32),
                    pltpu.SemaphoreType.DMA((2,)),
                ],
            ),
            out_shape=jax.ShapeDtypeStruct((beam_part, bands, 2, local_time * chan), jnp.bfloat16),
            input_output_aliases=alias,
            compiler_params=pltpu.CompilerParams(vmem_limit_bytes=VMEM),
            cost_estimate=pl.CostEstimate(
                flops=10_000_000_000, bytes_accessed=13_000_000, transcendentals=0
            ),
            name="synth",
        )(*operands)

    return result


def solution(mesh):
    in_specs = (P("sub", None, None, "tm"), P("sub", None, None, None), P(), P(), P(), P())
    out_specs = P("sub", None, None, "tm")
    return jax.shard_map(
        on_device, mesh=mesh, in_specs=in_specs, out_specs=out_specs, check_vma=False
    )
```

profile of v0, /device:TPU:7, one launch (start us, length us, event | category | flops | bytes accessed | tf_op | source)
XLA Modules:
  0.0 365.3 jit_solution(16210590570302864058)
XLA Ops:
  0.0 1.4 slice.55
  1.7 1.3 collective-permute-start
  4.4 1.8 fusion.perm_ref
  6.2 1.0 fusion.1.hot_ref
  7.2 2.4 copy.31.table_ref
  10.8 21.4 %form.2 = (bf16[12,512,128]{2,1,0:T(8,128)(2,1)}, bf16[16,12,8,8,128]{4,3,2,1,0:T(8,128)(2,1)}) custom-call(bf16[512,640]{1,0:T(8,128)(2,1)} %fusion.1.hot_ref, bf16[1024,1024]{1,0:T(8,128)(2,1)} %fusion.perm_ref, bf16[12,2,320,96]{3,2,1,0:T(8,128)(2,1)} %copy.31.table_ref, bf16[12,192,1024]{2,1,0:T(8,128)(2,1)} %bitcast.46, bf16[12,192,128]{2,1,0:T(8,128)(2,1)} %pad.4.rest_0_), custom_call_target="tpu_custom_call" | custom-call | flops 12000000000 | bytes 20000000 | tf_op jit(solution)/shard_map/form/pallas_call | solution.py:197
  32.2 2.2 slice.42
  34.5 1.9 fusion.21
  36.4 2.4 reshape.244
  38.8 1.9 reshape.243
  43.5 2.9 pad_maximum_fusion
  46.4 6.6 %all-to-all-start.1 = ((bf16[16,102,8,128]{3,2,1,0:T(8,128)(2,1)}), bf16[16,102,8,128]{3,2,1,0:T(8,128)(2,1)S(1)}, u32[]{:S(2)}, u32[]{:S(2)}) async-start(bf16[16,102,8,128]{3,2,1,0:T(8,128)(2,1)} %pad_maximum_fusion), calls=%async_computation.1 | async-start | bytes 6684672 | tf_op jit(solution)/shard_map/all_to_all | solution.py:249
  53.1 17.6 %form.3 = (bf16[16,12,8,16,128]{4,3,2,1,0:T(8,128)(2,1)}, bf16[16,12,8,8,128]{4,3,2,1,0:T(8,128)(2,1)}) custom-call(bf16[512,640]{1,0:T(8,128)(2,1)} %fusion.1.hot_ref, bf16[1024,1024]{1,0:T(8,128)(2,1)} %fusion.perm_ref, bf16[12,2,320,96]{3,2,1,0:T(8,128)(2,1)} %copy.31.table_ref, bf16[12,192,1024]{2,1,0:T(8,128)(2,1)} %bitcast.47), custom_call_target="tpu_custom_call" | custom-call | flops 12000000000 | bytes 20000000 | tf_op jit(solution)/shard_map/form/pallas_call | solution.py:197
  70.6 49.1 %all-to-all-done.1.z_ref = bf16[16,102,8,128]{3,2,1,0:T(8,128)(2,1)S(1)} async-done(((bf16[16,102,8,128]{3,2,1,0:T(8,128)(2,1)}), bf16[16,102,8,128]{3,2,1,0:T(8,128)(2,1)S(1)}, u32[]{:S(2)}, u32[]{:S(2)}) %all-to-all-start.1) | async-done | bytes 3342368 | tf_op jit(solution)/shard_map/all_to_all | solution.py:249
  119.7 149.6 %all_to_all.15.z_ref = bf16[16,96,16,128]{3,2,1,0:T(8,128)(2,1)} all-to-all(bf16[16,96,16,128]{3,2,1,0:T(8,128)(2,1)} %bitcast.39), channel_id=1, replica_groups=mesh['sub'=16,'tm'=2] {'sub'}, dimensions={0} | all-to-all | bytes 12582912 | tf_op jit(solution)/shard_map/all_to_all | solution.py:249
  269.3 5.3 %all-to-all-start = ((bf16[16,96,8,128]{3,2,1,0:T(8,128)(2,1)}), bf16[16,96,8,128]{3,2,1,0:T(8,128)(2,1)}, u32[]{:S(2)}, u32[]{:S(2)}) async-start(bf16[16,96,8,128]{3,2,1,0:T(8,128)(2,1)} %bitcast.42), calls=%async_computation | async-start | bytes 6291456 | tf_op jit(solution)/shard_map/all_to_all | solution.py:249
  277.3 3.7 %convert_element_type.78.mat_ref = bf16[768,256]{1,0:T(8,128)(2,1)} reshape(bf16[3,2,8,16,2,8,16]{6,5,4,3,2,1,0:T(8,128)(2,1)S(1)} %multiply_convert_fusion) | data formatting | bytes 786432 | tf_op jit(solution)/shard_map/convert_element_type | solution.py:40
  281.2 1.0 gather_fusion
  283.3 1.0 reshape.248.rim_ref
  286.4 1.6 copy.37
  288.1 2.7 reshape.251.rim_ref
  290.8 19.7 %synth.3.rest_0_ = bf16[16,12,2,16384]{3,2,1,0:T(2,128)(2,1)} custom-call(s32[192]{0:T(256)} %order_ref.5, s32[1]{0:T(128)} %copy.42.live_ref, bf16[16,102,8,128]{3,2,1,0:T(8,128)(2,1)} %copy-done.2, f32[12,4,2,2,128]{4,3,2,1,0:T(2,128)} %reshape.253.rim_ref, bf16[768,256]{1,0:T(8,128)(2,1)} %convert_element_type.78.mat_ref), custom_call_target="tpu_custom_call" | custom-call | flops 10000000000 | bytes 13000000 | tf_op jit(solution)/shard_map/synth/pallas_call | solution.py:275
  310.5 34.8 %synth.4.rest_0_ = bf16[16,12,2,16384]{3,2,1,0:T(2,128)(2,1)} custom-call(s32[192]{0:T(256)} %order_ref.5, s32[1]{0:T(128)} %copy.42.live_ref, bf16[16,96,16,128]{3,2,1,0:T(8,128)(2,1)} %all_to_all.15.z_ref, f32[12,8,2,2,128]{4,3,2,1,0:T(2,128)} %reshape.251.rim_ref, bf16[768,256]{1,0:T(8,128)(2,1)} %convert_element_type.78.mat_ref, ...), custom_call_target="tpu_custom_call", output_to_operand_aliasing={{}: (5, {})} | custom-call | flops 10000000000 | bytes 13000000 | tf_op jit(solution)/shard_map/synth/pallas_call | solution.py:275
  345.3 19.8 %synth.5 = bf16[16,12,2,16384]{3,2,1,0:T(2,128)(2,1)} custom-call(s32[192]{0:T(256)} %order_ref.5, s32[1]{0:T(128)} %copy.42.live_ref, bf16[16,96,8,128]{3,2,1,0:T(8,128)(2,1)} %all-to-all-done.z_ref, f32[12,4,2,2,128]{4,3,2,1,0:T(2,128)} %reshape.248.rim_ref, bf16[768,256]{1,0:T(8,128)(2,1)} %convert_element_type.78.mat_ref, ...), custom_call_target="tpu_custom_call", output_to_operand_aliasing={{}: (5, {})} | custom-call | flops 10000000000 | bytes 13000000 | tf_op jit(solution)/shard_map/synth/pallas_call | solution.py:275
  (64 shorter events, 11.0 us)
Async XLA Ops:
  0.0 275.7 %copy-start = (f32[16,16]{1,0:T(8,128)S(1)}, f32[16,16]{1,0:T(8,128)}, u32[]{:S(2)}) copy-start(f32[16,16]{1,0:T(8,128)} %param.11) | copy-start | bytes 3076
  0.0 7.2 %copy-start.4 = (bf16[12,2,320,96]{2,3,1,0:T(8,128)(2,1)S(1)}, bf16[12,2,320,96]{2,3,1,0:T(8,128)(2,1)}, u32[]{:S(2)}) copy-start(bf16[12,2,320,96]{2,3,1,0:T(8,128)(2,1)} %param.7) | copy-start | bytes 4423684
  1.7 7.9 %collective-permute-start = (bf16[12,192,16]{1,2,0:T(8,128)(2,1)S(1)}, bf16[12,192,16]{1,2,0:T(8,128)(2,1)S(1)}, u32[]{:S(2)}, u32[]{:S(2)}) collective-permute-start(bf16[12,192,16]{1,2,0:T(8,128)(2,1)S(1)} %copy.28), channel_id=1, source_target_pairs={{0,1},{2,3},{4,5},{6,7},{8,9},{10,11},{12,13},{14,15},{16,17},{18,... | collective-permute-start | bytes 221192 | tf_op jit(solution)/shard_map/ppermute | solution.py:175
  32.2 11.3 %copy-start.3 = (bf16[16,12,8,8,128]{4,3,2,1,0:T(8,128)(2,1)S(1)}, bf16[16,12,8,8,128]{4,3,2,1,0:T(8,128)(2,1)}, u32[]{:S(2)}) copy-start(bf16[16,12,8,8,128]{4,3,2,1,0:T(8,128)(2,1)} %get-tuple-element.10) | copy-start | bytes 9437188
  46.4 73.3 %all-to-all-start.1 = ((bf16[16,102,8,128]{3,2,1,0:T(8,128)(2,1)}), bf16[16,102,8,128]{3,2,1,0:T(8,128)(2,1)S(1)}, u32[]{:S(2)}, u32[]{:S(2)}) async-start(bf16[16,102,8,128]{3,2,1,0:T(8,128)(2,1)} %pad_maximum_fusion), calls=%async_computation.1 | async-start | bytes 6684672 | tf_op jit(solution)/shard_map/all_to_all | solution.py:249
  119.7 149.6 %copy-start.2 = (bf16[16,102,8,128]{3,2,1,0:T(8,128)(2,1)}, bf16[16,102,8,128]{3,2,1,0:T(8,128)(2,1)S(1)}, u32[]{:S(2)}) copy-start(bf16[16,102,8,128]{3,2,1,0:T(8,128)(2,1)S(1)} %all-to-all-done.1.z_ref) | copy-start | bytes 10027012
  269.3 76.0 %all-to-all-start = ((bf16[16,96,8,128]{3,2,1,0:T(8,128)(2,1)}), bf16[16,96,8,128]{3,2,1,0:T(8,128)(2,1)}, u32[]{:S(2)}, u32[]{:S(2)}) async-start(bf16[16,96,8,128]{3,2,1,0:T(8,128)(2,1)} %bitcast.42), calls=%async_computation | async-start | bytes 6291456 | tf_op jit(solution)/shard_map/all_to_all | solution.py:249
  276.5 4.5 %copy-start.5 = (s32[192]{0:T(256)S(1)}, s32[192]{0:T(256)}, u32[]{:S(2)}) copy-start(s32[192]{0:T(256)} %order_ref.5) | copy-start | bytes 2308
  276.5 4.5 %slice-start = ((bf16[16,102,8,128]{3,2,1,0:T(8,128)(2,1)}), bf16[16,6,8,128]{3,2,1,0:T(8,128)(2,1)S(1)}, s32[]{:S(2)}) async-start(bf16[16,102,8,128]{3,2,1,0:T(8,128)(2,1)} %copy-done.2), calls=%async_computation.3 | async-start | bytes 393216 | tf_op jit(solution)/shard_map/slice | solution.py:250
  345.3 19.8 %copy-start.1 = (f32[16,16]{1,0:T(8,128)S(1)}, f32[16,16]{1,0:T(8,128)}, u32[]{:S(2)}) copy-start(f32[16,16]{1,0:T(8,128)} %param.11) | copy-start | bytes 3076
where the time goes:
time: 369 us; the launch traced here: 365 us
  blocking collectives  150 us (41%)
  Pallas kernels  113 us (31%)
  waiting for transfers between devices  49.1 us (13%)
  local copies, waits for them, and re-layouts  30.9 us (8%)
  starting transfers between devices  13.3 us (4%)
  other arithmetic  8.07 us (2%)
    all_to_all x1, blocking collectives, on_device(): lax.all_to_all(p, 'sub', split_axis=0, concat_axis=0, tiled=True)  150 us
    pallas_call x3, Pallas kernels, on_device(): pl.pallas_call(functools.partial(synth_kernel, inner, chan, group, reach,...  74.3 us
    all_to_all x2, waiting for transfers between devices, on_device(): lax.all_to_all(p, 'sub', split_axis=0, concat_axis=0, tiled=True)  49.1 us
    pallas_call x2, Pallas kernels, form(): pl.pallas_call(functools.partial(form_kernel, inner, groups, with_rim), g...  39 us
    all_to_all x2, starting transfers between devices, on_device(): lax.all_to_all(p, 'sub', split_axis=0, concat_axis=0, tiled=True)  12 us
  transfers between devices with their start and end apart: 3, of which 1 were waited for; matrix products, arithmetic and copies ran while one was open for 6% of the time, Pallas kernels for 20%

commit v1 on v0

--- a/solution.py
+++ b/solution.py
@@ -149,7 +149,7 @@
     lax.fori_loop(0, group // 2, emit, 0)
 
 
-def on_device(voltages, pointing_table, beam_pointing, subband_order, live_subbands, filter_taps):
+def direct_plan(voltages, pointing_table, beam_pointing, subband_order, live_subbands, filter_taps):
     local_subbands, _, inputs, local_time = voltages.shape
     pointings = pointing_table.shape[2]
     beam_count = beam_pointing.shape[0]
@@ -301,6 +301,522 @@
 
     return result
 
+MESH = pl.DeviceIdType.MESH
+
+
+def drain(ref, sem):
+    pltpu.make_async_copy(ref, ref, sem).wait()
+
+
+def relay_kernel(
+    n,
+    chan,
+    order_ref,
+    live_ref,
+    pick_ref,
+    table_ref,
+    taps_ref,
+    trig_ref,
+    volt_ref,
+    out_ref,
+    z,
+    own_out,
+    far_out,
+    volts,
+    far_volts,
+    chosen,
+    far_chosen,
+    own_w,
+    far_w,
+    lhs,
+    stage,
+    wide,
+    line,
+    mat,
+    made,
+    ready,
+    tail,
+    tail_sent,
+    rim,
+    z_sem,
+    own_sem,
+    far_sem,
+    in_sem,
+    volt_send,
+    volt_recv,
+    w_send,
+    w_recv,
+    fwd_send,
+    fwd_recv,
+    rim_sem,
+    out_sem,
+):
+    f32, bf16 = jnp.float32, jnp.bfloat16
+    half, quarter = n // 2, n // 4
+    chunks, slots_here, inputs2, _ = volts.shape
+    pair = z.shape[2]
+    group = pair // 2
+    bands = ready.shape[1]
+    inner = LANES // chan
+    spans = mat.shape[0] // pair_of(chan)
+    halo = spans - inner
+    blocks = LANES // inner
+    ring = far_out.shape[0]
+
+    me, tm = lax.axis_index("sub"), lax.axis_index("tm")
+    side, pos = lax.div(me, half), lax.rem(me, half)
+    rank, lane = lax.div(pos, quarter), lax.rem(me, quarter)
+    other = 1 - side
+    is_gate = rank == 1 - side
+    gate = other * half + side * quarter + lane
+    share = slots_here // 2
+    mine = pl.ds(tm * share, share)
+    theirs = pl.ds((1 - tm) * share, share)
+
+    def chunk_at(step):
+        return lax.rem(step + chunks - 1, chunks)
+
+    def source_of(rank_from):
+        return other * half + rank_from * quarter + lane
+
+    def load(c):
+        return pltpu.make_async_copy(
+            volt_ref.at[:, :, pl.ds(pl.multiple_of(c * LANES, LANES), LANES)],
+            volts.at[c],
+            in_sem.at[c],
+        )
+
+    def send_volts(c):
+        pltpu.make_async_remote_copy(
+            src_ref=volts.at[c],
+            dst_ref=far_volts.at[c, rank],
+            send_sem=volt_send.at[c],
+            recv_sem=volt_recv.at[c, rank],
+            device_id=(gate, tm),
+            device_id_type=MESH,
+        ).start()
+
+    def send_all(sent, src, c, sems):
+        def to(j, carry):
+            there = lax.rem(pos + 1 + j, half)
+            pltpu.make_async_remote_copy(
+                src_ref=sent.at[there],
+                dst_ref=z.at[c, pl.ds(src * slots_here, slots_here)],
+                send_sem=sems.at[there],
+                recv_sem=z_sem.at[c, src],
+                device_id=(side * half + there, tm),
+                device_id_type=MESH,
+            ).start()
+            return carry
+
+        lax.fori_loop(0, half - 1, to, 0)
+
+    def wait_all(sent, sems):
+        def one(j, carry):
+            there = lax.rem(pos + 1 + j, half)
+            drain(sent.at[there], sems.at[there])
+            return carry
+
+        lax.fori_loop(0, half - 1, one, 0)
+
+    def form(weights, signal, sent, src, c):
+        def one(s, carry):
+            formed = jnp.dot(
+                weights[s][:, :inputs2], signal[s], preferred_element_type=f32
+            ).astype(bf16)
+            for d in range(half):
+                sent[d, s] = formed[d * pair : (d + 1) * pair]
+            return carry
+
+        lax.fori_loop(0, slots_here, one, 0)
+
+        def keep(s, carry):
+            z[c, src * slots_here + s] = sent[pos, s]
+            return carry
+
+        lax.fori_loop(0, slots_here, keep, 0)
+
+    def prepare(picked, weights, at):
+        w = picked.astype(f32)
+        real, imag = w[: inputs2 // 2], w[inputs2 // 2 :]
+        rest = jnp.zeros((weights.shape[2] - inputs2, LANES), f32)
+        upper = jnp.concatenate([real, -imag, rest], axis=0).T.astype(bf16)
+        lower = jnp.concatenate([imag, real, rest], axis=0).T.astype(bf16)
+        for d in range(half):
+            rows = slice(d * group, (d + 1) * group)
+            weights[at, d * pair : d * pair + group] = upper[rows]
+            weights[at, d * pair + group : (d + 1) * pair] = lower[rows]
+
+    for step in range(chunks):
+        load(chunk_at(step)).start()
+    load(chunk_at(0)).wait()
+    send_volts(chunk_at(0))
+
+    pointings = table_ref.shape[2]
+    hot = (
+        lax.broadcasted_iota(jnp.int32, (pointings, 2 * LANES), 0) == pick_ref[...]
+    ).astype(bf16)
+
+    def choose(s, carry):
+        picked = jnp.dot(table_ref[s], hot, preferred_element_type=f32).astype(bf16)
+        chosen[0, s] = picked[:, :LANES]
+        chosen[1, s] = picked[:, LANES:]
+        return carry
+
+    lax.fori_loop(0, slots_here, choose, 0)
+    pltpu.make_async_remote_copy(
+        src_ref=chosen.at[other, mine],
+        dst_ref=far_chosen.at[rank, mine],
+        send_sem=w_send,
+        recv_sem=w_recv.at[rank],
+        device_id=(gate, tm),
+        device_id_type=MESH,
+    ).start()
+    load(chunk_at(1)).wait()
+    send_volts(chunk_at(1))
+
+    def prepare_own(s, carry):
+        prepare(chosen[side, s], own_w, s)
+        return carry
+
+    lax.fori_loop(0, slots_here, prepare_own, 0)
+
+    for v in range(spans):
+        taps = taps_ref[v : v + 1, :]
+        mat[v * 2 * chan : (v + 1) * 2 * chan] = (
+            jnp.concatenate([taps, taps], axis=1) * trig_ref[...]
+        ).astype(bf16)
+    tail[...] = jnp.zeros_like(tail)
+
+    def foreign_weights():
+        def forward(k):
+            return pltpu.make_async_remote_copy(
+                src_ref=far_chosen.at[k, mine],
+                dst_ref=far_chosen.at[k, mine],
+                send_sem=fwd_send.at[k],
+                recv_sem=fwd_recv.at[k],
+                device_id=(me, 1 - tm),
+                device_id_type=MESH,
+            )
+
+        for k in range(2):
+            drain(far_chosen.at[k, mine], w_recv.at[k])
+            forward(k).start()
+        for k in range(2):
+            drain(far_chosen.at[k, theirs], fwd_recv.at[k])
+        for k in range(2):
+
+            def one(s, carry):
+                prepare(far_chosen[k, s], far_w.at[k], s)
+                return carry
+
+            lax.fori_loop(0, slots_here, one, 0)
+        for k in range(2):
+            drain(far_chosen.at[k, mine], fwd_send.at[k])
+
+    lanes_at = lax.broadcasted_iota(jnp.int32, (blocks, LANES), 1)
+    width = 2 * chan
+    fold = LANES // width
+
+    def synthesise(i):
+        c = chunk_at(lax.rem(i - 1, chunks))
+
+        @pl.when(i <= chunks)
+        def _():
+            def one(src, carry):
+                local = (src == me) | (
+                    is_gate & (lax.div(src, half) == other) & (lax.rem(src, quarter) == lane)
+                )
+
+                @pl.when(jnp.logical_not(local))
+                def _():
+                    drain(z.at[c, pl.ds(src * slots_here, slots_here)], z_sem.at[c, src])
+
+                return carry
+
+            lax.fori_loop(0, n, one, 0)
+
+        def copy(s, carry):
+            stage[s] = z[c, s]
+            return carry
+
+        lax.fori_loop(0, stage.shape[0], copy, 0, unroll=4)
+
+        def gather(g, carry):
+            for k in range(chan):
+                alive = g * chan + k < live_ref[0]
+                block = stage[order_ref[g * chan + k]].astype(f32)
+                wide[k * pair : (k + 1) * pair] = jnp.where(alive, block, 0.0)
+
+            def turn(q, carry):
+                rows = [
+                    wide[pl.ds(p * group + q * fold + b, chan, stride=pair), :]
+                    for b in range(fold)
+                    for p in range(2)
+                ]
+                turned = jnp.concatenate(rows, axis=0).T
+                at = g * (group // fold) + q
+                line[:halo] = tail[at]
+                line[halo : halo + LANES] = turned
+                tail[at] = turned[LANES - halo :]
+                for u in range(spans // fold):
+                    parts = [
+                        line[pl.ds(u * fold + w, blocks, stride=inner), :] for w in range(fold)
+                    ]
+                    for b in range(fold):
+                        block = None
+                        for w in range(fold):
+                            shift = (w - b) * width % LANES
+                            part = pltpu.roll(parts[w], shift, 1) if shift else parts[w]
+                            if block is None:
+                                block = part
+                            else:
+                                block = jnp.where(lanes_at >= w * width, part, block)
+                        lhs[
+                            q * fold + b,
+                            pl.ds(pl.multiple_of(g * blocks, blocks), blocks),
+                            u * LANES : (u + 1) * LANES,
+                        ] = block.astype(bf16)
+                return carry
+
+            lax.fori_loop(0, group // fold, turn, 0)
+            return carry
+
+        lax.fori_loop(0, bands, gather, 0)
+
+        out_copy = pltpu.make_async_copy(
+            ready,
+            out_ref.at[:, :, pl.ds(pl.multiple_of(c * 2 * blocks, 2 * blocks), 2 * blocks)],
+            out_sem,
+        )
+
+        @pl.when(i > 1)
+        def _():
+            drain(ready, out_sem)
+
+        def emit(b, carry):
+            out = jnp.dot(lhs[b], mat[...], preferred_element_type=f32)
+            rows = bands * blocks
+            made[pl.ds(0, rows, stride=2), :] = out[:, :LANES]
+            made[pl.ds(1, rows, stride=2), :] = out[:, LANES:]
+            for g in range(bands):
+                ready[b, g] = made[g * 2 * blocks : (g + 1) * 2 * blocks].astype(bf16)
+            return carry
+
+        lax.fori_loop(0, group, emit, 0)
+        out_copy.start()
+
+    def pass_tail():
+        return pltpu.make_async_remote_copy(
+            src_ref=tail_sent,
+            dst_ref=rim,
+            send_sem=rim_sem.at[0],
+            recv_sem=rim_sem.at[1],
+            device_id=(me, 1),
+            device_id_type=MESH,
+        )
+
+    def step(i, carry):
+        c = chunk_at(i)
+
+        @pl.when(i + 2 < chunks)
+        def _():
+            later = chunk_at(i + 2)
+            load(later).wait()
+            send_volts(later)
+
+        @pl.when(i < chunks)
+        def _():
+            form(own_w, volts.at[c], own_out.at[c], me, c)
+            send_all(own_out.at[c], me, c, own_sem.at[c])
+
+        @pl.when(is_gate & (i == 0))
+        def _():
+            foreign_weights()
+
+        @pl.when(is_gate & (i < chunks))
+        def _():
+            turn = lax.rem(i, ring)
+
+            def one(k, carry):
+                @pl.when(i >= ring)
+                def _():
+                    wait_all(far_out.at[turn, k], far_sem.at[turn, k])
+
+                drain(far_volts.at[c, k], volt_recv.at[c, k])
+                src = source_of(k)
+                form(far_w.at[k], far_volts.at[c, k], far_out.at[turn, k], src, c)
+                send_all(far_out.at[turn, k], src, c, far_sem.at[turn, k])
+                return carry
+
+            lax.fori_loop(0, 2, one, 0)
+
+        @pl.when((i == 2) & (tm == 0))
+        def _():
+            tail[...] = jnp.zeros_like(tail)
+
+        @pl.when((i == 2) & (tm == 1))
+        def _():
+            drain(rim, rim_sem.at[1])
+            tail[...] = rim[...]
+
+        @pl.when(i >= 1)
+        def _():
+            synthesise(i)
+
+        @pl.when((i == 1) & (tm == 0))
+        def _():
+            tail_sent[...] = tail[...]
+            pass_tail().start()
+
+        return carry
+
+    lax.fori_loop(0, chunks + 2, step, 0)
+
+    drain(ready, out_sem)
+    drain(chosen.at[other, mine], w_send)
+
+    @pl.when(tm == 0)
+    def _():
+        drain(tail_sent, rim_sem.at[0])
+
+    def finish(c, carry):
+        drain(volts.at[c], volt_send.at[c])
+        wait_all(own_out.at[c], own_sem.at[c])
+        return carry
+
+    lax.fori_loop(0, chunks, finish, 0)
+
+    @pl.when(is_gate)
+    def _():
+        def one(turn, carry):
+            for k in range(2):
+                wait_all(far_out.at[turn, k], far_sem.at[turn, k])
+            return carry
+
+        lax.fori_loop(0, ring, one, 0)
+
+
+def pair_of(chan):
+    return 2 * chan
+
+
+def relay_plan(voltages, pointing_table, beam_pointing, subband_order, live_subbands, filter_taps):
+    local, _, inputs, local_time = voltages.shape
+    pointings = pointing_table.shape[2]
+    beams = beam_pointing.shape[0]
+    slots = subband_order.shape[0]
+    tap_count, chan = filter_taps.shape
+    n = lax.axis_size("sub")
+    half = n // 2
+    group = beams // n
+    pair = 2 * group
+    inner = LANES // chan
+    spans = inner * (1 + -(-(tap_count - 1) // inner))
+    halo = spans - inner
+    chunks = local_time // LANES
+    bands = slots // chan
+    blocks = LANES // inner
+    fold = LANES // (2 * chan)
+    bf16, f32 = jnp.bfloat16, jnp.float32
+    ring = 2
+
+    flat = filter_taps.reshape(-1)
+    before, after = (inner - 1) * chan, halo * chan + LANES - flat.shape[0]
+    flat = jnp.pad(flat, (before, after))
+    taps = jnp.stack(
+        [
+            flat[before + chan * (halo - v) : before + chan * (halo - v) + LANES]
+            for v in range(spans)
+        ]
+    )
+    trig = inverse_table(chan).astype(f32).transpose(2, 3, 0, 1)
+    trig = jnp.broadcast_to(trig[:, :, :, None, :], (2, chan, 2, inner, chan))
+    trig = trig.reshape(2 * chan, 2 * LANES)
+    signal = voltages.reshape(local, 2 * inputs, local_time)
+    table = pointing_table.transpose(0, 1, 3, 2).reshape(local, 2 * inputs, pointings)
+    lanes_in = 2 * LANES
+
+    vmem = pl.BlockSpec(memory_space=pltpu.VMEM)
+    smem = pl.BlockSpec(memory_space=pltpu.SMEM)
+    anywhere = pl.BlockSpec(memory_space=pl.ANY)
+    dma = pltpu.SemaphoreType.DMA
+    out = pl.pallas_call(
+        functools.partial(relay_kernel, n, chan),
+        in_specs=[smem, smem, vmem, vmem, vmem, vmem, anywhere],
+        out_specs=anywhere,
+        out_shape=jax.ShapeDtypeStruct((group, bands, 2 * blocks * chunks, LANES), bf16),
+        scratch_shapes=[
+            pltpu.VMEM((chunks, slots, pair, LANES), bf16),
+            pltpu.VMEM((chunks, half, local, pair, LANES), bf16),
+            pltpu.VMEM((ring, 2, half, local, pair, LANES), bf16),
+            pltpu.VMEM((chunks, local, 2 * inputs, LANES), bf16),
+            pltpu.VMEM((chunks, 2, local, 2 * inputs, LANES), bf16),
+            pltpu.VMEM((2, local, 2 * inputs, LANES), bf16),
+            pltpu.VMEM((2, local, 2 * inputs, LANES), bf16),
+            pltpu.VMEM((local, half * pair, lanes_in), bf16),
+            pltpu.VMEM((2, local, half * pair, lanes_in), bf16),
+            pltpu.VMEM((group, bands * blocks, spans * 2 * chan), bf16),
+            pltpu.VMEM((slots, pair, LANES), bf16),
+            pltpu.VMEM((chan * pair, LANES), f32),
+            pltpu.VMEM((halo + LANES, LANES), f32),
+            pltpu.VMEM((spans * 2 * chan, 2 * LANES), bf16),
+            pltpu.VMEM((bands * blocks * 2, LANES), f32),
+            pltpu.VMEM((group, bands, 2 * blocks, LANES), bf16),
+            pltpu.VMEM((bands * group // fold, halo, LANES), f32),
+            pltpu.VMEM((bands * group // fold, halo, LANES), f32),
+            pltpu.VMEM((bands * group // fold, halo, LANES), f32),
+            dma((chunks, n)),
+            dma((chunks, half)),
+            dma((ring, 2, half)),
+            dma((chunks,)),
+            dma((chunks,)),
+            dma((chunks, 2)),
+            dma,
+            dma((2,)),
+            dma((2,)),
+            dma((2,)),
+            dma((2,)),
+            dma,
+        ],
+        compiler_params=pltpu.CompilerParams(
+            vmem_limit_bytes=66_000_000, has_side_effects=True
+        ),
+        cost_estimate=pl.CostEstimate(
+            flops=20_000_000_000, bytes_accessed=20_000_000, transcendentals=0
+        ),
+        name="relay",
+    )(
+        subband_order,
+        live_subbands,
+        beam_pointing.reshape(1, beams),
+        table,
+        taps,
+        trig,
+        signal,
+    )
+    out = out.reshape(group, bands, blocks * chunks, 2, LANES).transpose(0, 1, 3, 2, 4)
+    return out.reshape(group, bands, 2, local_time * chan)
+
+
+def on_device(voltages, pointing_table, beam_pointing, subband_order, live_subbands, filter_taps):
+    local, _, inputs, local_time = voltages.shape
+    beams = beam_pointing.shape[0]
+    n = lax.axis_size("sub")
+    fits = (
+        lax.axis_size("tm") == 2
+        and n % 4 == 0
+        and beams == 2 * LANES
+        and beams // n % 8 == 0
+        and local % 2 == 0
+        and local_time % LANES == 0
+        and local_time >= 4 * LANES
+    )
+    plan = relay_plan if fits else direct_plan
+    return plan(
+        voltages, pointing_table, beam_pointing, subband_order, live_subbands, filter_taps
+    )
+
 
 def solution(mesh):
     in_specs = (P("sub", None, None, "tm"), P("sub", None, None, None), P(), P(), P(), P())

time: 369 us -> 361 us (0.978); the launches traced: 365 us -> 361 us
  Pallas kernels: 113 us -> 344 us
  blocking collectives: 150 us -> 0 us
  waiting for transfers between devices: 49.1 us -> 0 us
  local copies, waits for them, and re-layouts: 30.9 us -> 16.7 us
  starting transfers between devices: 13.3 us -> 0 us
  other arithmetic: 8.07 us -> 0.15 us
    pallas_call x5 -> x1, Pallas kernels: 113 us -> 344 us  [relay_plan(): pl.pallas_call(functools.partial(relay_kernel, n, chan), in_specs=[smem,...]
    all_to_all x1 -> x0, blocking collectives: 150 us -> none  [on_device(): lax.all_to_all(p, 'sub', split_axis=0, concat_axis=0, tiled=True)]
    all_to_all x2 -> x0, waiting for transfers between devices: 49.1 us -> none  [on_device(): lax.all_to_all(p, 'sub', split_axis=0, concat_axis=0, tiled=True)]
    all_to_all x2 -> x0, starting transfers between devices: 12 us -> none  [on_device(): lax.all_to_all(p, 'sub', split_axis=0, concat_axis=0, tiled=True)]
    reshape x11 -> x2, local copies, waits for them, and re-layouts: 12.7 us -> 1.54 us  [the longest x1 0.78 us: relay_plan(): flat = filter_taps.reshape(-1)]
    unnamed x13 -> x1, local copies, waits for them, and re-layouts: 2.38 us -> 11.4 us
    slice x13 -> x1, local copies, waits for them, and re-layouts: 6.33 us -> 1 us  [relay_plan(): flat[before + chan * (halo - v):before + chan * (halo - v) + LANES]]
  transfers between devices with their start and end apart: 3 -> 0, of which waited for: 1 -> 0; matrix products, arithmetic and copies ran while one was open for 6% -> 0% of each run, Pallas kernels for 20% -> 0%
where the time goes in v1:
time: 361 us
  Pallas kernels  344 us (95%)
  local copies, waits for them, and re-layouts  16.7 us (5%)
    pallas_call x1, Pallas kernels, relay_plan(): pl.pallas_call(functools.partial(relay_kernel, n, chan), in_specs=[smem,...  344 us
    unnamed x1, local copies, waits for them, and re-layouts  11.4 us

profile of v1, /device:TPU:7, one launch (start us, length us, event | category | flops | bytes accessed | tf_op | source)
XLA Modules:
  0.0 361.1 jit_solution(13936982673095025597)
XLA Ops:
  0.7 0.8 reshape.123
  1.4 0.1 fusion.6
  1.5 0.1 fusion.20
  1.6 0.1 sine_convert_fusion
  1.7 0.1 copy.9
  1.8 1.0 fusion.21
  2.8 0.1 stack.110
  2.8 0.1 stack.108
  2.9 0.1 stack.107
  3.0 0.1 stack.106
  3.1 0.1 stack.105
  3.2 0.1 stack.104
  3.2 0.1 stack.103
  3.3 0.1 stack.102
  3.4 0.1 stack.109
  3.5 1.8 stack.118.taps_ref
  5.4 0.8 reshape.124.trig_ref
  6.1 343.6 %relay.1 = bf16[16,12,256,128]{3,2,1,0:T(8,128)(2,1)} custom-call(s32[192]{0:T(256)} %order_ref.1, s32[1]{0:T(128)S(6)} %copy.12.live_ref, s32[1,256]{1,0:T(1,128)} %bitcast.49, bf16[12,192,320]{2,1,0:T(8,128)(2,1)} %bitcast.48, f32[24,128]{1,0:T(8,128)} %stack.118.taps_ref, f32[32,256]{1,0:T(8,128)} %reshape.124.trig_ref, bf16[12,192,1024]{2,1,0:T(8,128)(2,1)} %bitcast.47), custom_call_target="tpu_custom_call" | custom-call | flops 20000000000 | bytes 20000000 | tf_op jit(solution)/shard_map/relay/pallas_call | solution.py:744
  349.8 11.4 %copy.13 = bf16[16,12,2,16384]{3,2,1,0:T(2,128)(2,1)} copy(bf16[16,12,2,16384]{3,2,1,0:T(2,128)(2,1)} %bitcast.46) | data formatting | bytes 25165824
  (4 shorter events, 0.0 us)

commit v2 on v1

--- a/solution.py
+++ b/solution.py
@@ -332,6 +332,7 @@
     stage,
     wide,
     line,
+    steps,
     mat,
     made,
     ready,
@@ -368,6 +369,7 @@
     rank, lane = lax.div(pos, quarter), lax.rem(me, quarter)
     other = 1 - side
     is_gate = rank == 1 - side
+    near = side
     gate = other * half + side * quarter + lane
     share = slots_here // 2
     mine = pl.ds(tm * share, share)
@@ -428,7 +430,7 @@
                 sent[d, s] = formed[d * pair : (d + 1) * pair]
             return carry
 
-        lax.fori_loop(0, slots_here, one, 0)
+        lax.fori_loop(0, slots_here, one, 0, unroll=4)
 
         def keep(s, carry):
             z[c, src * slots_here + s] = sent[pos, s]
@@ -449,8 +451,13 @@
 
     for step in range(chunks):
         load(chunk_at(step)).start()
-    load(chunk_at(0)).wait()
-    send_volts(chunk_at(0))
+
+    def send_later(step, carry):
+        load(chunk_at(step)).wait()
+        send_volts(chunk_at(step))
+        return carry
+
+    send_later(0, 0)
 
     pointings = table_ref.shape[2]
     hot = (
@@ -464,16 +471,19 @@
         return carry
 
     lax.fori_loop(0, slots_here, choose, 0)
-    pltpu.make_async_remote_copy(
-        src_ref=chosen.at[other, mine],
-        dst_ref=far_chosen.at[rank, mine],
-        send_sem=w_send,
-        recv_sem=w_recv.at[rank],
-        device_id=(gate, tm),
-        device_id_type=MESH,
-    ).start()
-    load(chunk_at(1)).wait()
-    send_volts(chunk_at(1))
+
+    def send_weights():
+        pltpu.make_async_remote_copy(
+            src_ref=chosen.at[other, mine],
+            dst_ref=far_chosen.at[rank, mine],
+            send_sem=w_send,
+            recv_sem=w_recv.at[rank],
+            device_id=(gate, tm),
+            device_id_type=MESH,
+        ).start()
+
+    send_weights()
+    lax.fori_loop(1, chunks, send_later, 0)
 
     def prepare_own(s, carry):
         prepare(chosen[side, s], own_w, s)
@@ -488,35 +498,57 @@
         ).astype(bf16)
     tail[...] = jnp.zeros_like(tail)
 
-    def foreign_weights():
-        def forward(k):
-            return pltpu.make_async_remote_copy(
-                src_ref=far_chosen.at[k, mine],
-                dst_ref=far_chosen.at[k, mine],
-                send_sem=fwd_send.at[k],
-                recv_sem=fwd_recv.at[k],
-                device_id=(me, 1 - tm),
-                device_id_type=MESH,
-            )
-
-        for k in range(2):
-            drain(far_chosen.at[k, mine], w_recv.at[k])
-            forward(k).start()
-        for k in range(2):
-            drain(far_chosen.at[k, theirs], fwd_recv.at[k])
-        for k in range(2):
-
-            def one(s, carry):
-                prepare(far_chosen[k, s], far_w.at[k], s)
-                return carry
-
-            lax.fori_loop(0, slots_here, one, 0)
-        for k in range(2):
-            drain(far_chosen.at[k, mine], fwd_send.at[k])
-
-    lanes_at = lax.broadcasted_iota(jnp.int32, (blocks, LANES), 1)
+    def foreign_weights(k):
+        forward = pltpu.make_async_remote_copy(
+            src_ref=far_chosen.at[k, mine],
+            dst_ref=far_chosen.at[k, mine],
+            send_sem=fwd_send.at[k],
+            recv_sem=fwd_recv.at[k],
+            device_id=(me, 1 - tm),
+            device_id_type=MESH,
+        )
+        drain(far_chosen.at[k, mine], w_recv.at[k])
+        forward.start()
+        drain(far_chosen.at[k, theirs], fwd_recv.at[k])
+
+        def one(s, carry):
+            prepare(far_chosen[k, s], far_w.at[k], s)
+            return carry
+
+        lax.fori_loop(0, slots_here, one, 0)
+        drain(far_chosen.at[k, mine], fwd_send.at[k])
+
+    def foreign(k, i, turn):
+        c = chunk_at(i)
+        slot = lax.rem(turn, ring)
+
+        @pl.when(i == 0)
+        def _():
+            foreign_weights(k)
+
+        @pl.when(turn >= ring)
+        def _():
+            wait_all(far_out.at[slot], far_sem.at[slot])
+
+        drain(far_volts.at[c, k], volt_recv.at[c, k])
+        form(far_w.at[k], far_volts.at[c, k], far_out.at[slot], source_of(k), c)
+        send_all(far_out.at[slot], source_of(k), c, far_sem.at[slot])
+
     width = 2 * chan
     fold = LANES // width
+    lanes_at = lax.broadcasted_iota(jnp.int32, (LANES // fold, LANES), 1)
+
+    def swap(one, two, size):
+        low = lax.rem(lanes_at, 2 * size) < size
+        return (
+            jnp.where(low, one, pltpu.roll(two, size, 1)),
+            jnp.where(low, pltpu.roll(one, LANES - size, 1), two),
+        )
+
+    def exchange(parts):
+        first, third = swap(parts[0], parts[2], 2 * width)
+        second, fourth = swap(parts[1], parts[3], 2 * width)
+        return swap(first, second, width) + swap(third, fourth, width)
 
     def synthesise(i):
         c = chunk_at(lax.rem(i - 1, chunks))
@@ -548,38 +580,28 @@
                 block = stage[order_ref[g * chan + k]].astype(f32)
                 wide[k * pair : (k + 1) * pair] = jnp.where(alive, block, 0.0)
 
-            def turn(q, carry):
+            for q in range(group // fold):
                 rows = [
                     wide[pl.ds(p * group + q * fold + b, chan, stride=pair), :]
                     for b in range(fold)
                     for p in range(2)
                 ]
-                turned = jnp.concatenate(rows, axis=0).T
-                at = g * (group // fold) + q
-                line[:halo] = tail[at]
-                line[halo : halo + LANES] = turned
-                tail[at] = turned[LANES - halo :]
-                for u in range(spans // fold):
-                    parts = [
-                        line[pl.ds(u * fold + w, blocks, stride=inner), :] for w in range(fold)
-                    ]
-                    for b in range(fold):
-                        block = None
-                        for w in range(fold):
-                            shift = (w - b) * width % LANES
-                            part = pltpu.roll(parts[w], shift, 1) if shift else parts[w]
-                            if block is None:
-                                block = part
-                            else:
-                                block = jnp.where(lanes_at >= w * width, part, block)
+                line[q] = jnp.concatenate(rows, axis=0).T
+                split = [line[q, pl.ds(w, LANES // fold, stride=fold), :] for w in range(fold)]
+                for b, block in enumerate(exchange(split)):
+                    beam = q * fold + b
+                    at = g * group + beam
+                    steps[beam, :8] = tail[at]
+                    steps[beam, 8:] = block
+                    tail[at] = block[LANES // fold - 8 :]
+                    for e in range(spans // fold):
                         lhs[
-                            q * fold + b,
+                            beam,
                             pl.ds(pl.multiple_of(g * blocks, blocks), blocks),
-                            u * LANES : (u + 1) * LANES,
-                        ] = block.astype(bf16)
-                return carry
-
-            lax.fori_loop(0, group // fold, turn, 0)
+                            e * LANES : (e + 1) * LANES,
+                        ] = steps[
+                            beam, pl.ds(8 - halo // fold + e, blocks, stride=inner // fold), :
+                        ].astype(bf16)
             return carry
 
         lax.fori_loop(0, bands, gather, 0)
@@ -590,21 +612,24 @@
             out_sem,
         )
 
-        @pl.when(i > 1)
+        @pl.when(i > 2)
         def _():
             drain(ready, out_sem)
 
         def emit(b, carry):
             out = jnp.dot(lhs[b], mat[...], preferred_element_type=f32)
             rows = bands * blocks
-            made[pl.ds(0, rows, stride=2), :] = out[:, :LANES]
-            made[pl.ds(1, rows, stride=2), :] = out[:, LANES:]
+            turn = lax.rem(b, 2)
+            made[turn, pl.ds(0, rows, stride=2), :] = out[:, :LANES]
+            made[turn, pl.ds(1, rows, stride=2), :] = out[:, LANES:]
             for g in range(bands):
-                ready[b, g] = made[g * 2 * blocks : (g + 1) * 2 * blocks].astype(bf16)
+                ready[b, g] = made[turn, g * 2 * blocks : (g + 1) * 2 * blocks].astype(bf16)
             return carry
 
-        lax.fori_loop(0, group, emit, 0)
-        out_copy.start()
+        @pl.when(i > 1)
+        def _():
+            lax.fori_loop(0, group, emit, 0, unroll=2)
+            out_copy.start()
 
     def pass_tail():
         return pltpu.make_async_remote_copy(
@@ -616,49 +641,39 @@
             device_id_type=MESH,
         )
 
+    def early(i, carry):
+        c = chunk_at(i)
+
+        form(own_w, volts.at[c], own_out.at[c], me, c)
+        send_all(own_out.at[c], me, c, own_sem.at[c])
+
+        @pl.when(is_gate)
+        def _():
+            foreign(1 - near, i, i)
+
+        return carry
+
+    lax.fori_loop(0, chunks, early, 0)
+
     def step(i, carry):
-        c = chunk_at(i)
-
-        @pl.when(i + 2 < chunks)
-        def _():
-            later = chunk_at(i + 2)
-            load(later).wait()
-            send_volts(later)
-
-        @pl.when(i < chunks)
-        def _():
-            form(own_w, volts.at[c], own_out.at[c], me, c)
-            send_all(own_out.at[c], me, c, own_sem.at[c])
-
-        @pl.when(is_gate & (i == 0))
-        def _():
-            foreign_weights()
-
         @pl.when(is_gate & (i < chunks))
         def _():
-            turn = lax.rem(i, ring)
-
-            def one(k, carry):
-                @pl.when(i >= ring)
-                def _():
-                    wait_all(far_out.at[turn, k], far_sem.at[turn, k])
-
-                drain(far_volts.at[c, k], volt_recv.at[c, k])
-                src = source_of(k)
-                form(far_w.at[k], far_volts.at[c, k], far_out.at[turn, k], src, c)
-                send_all(far_out.at[turn, k], src, c, far_sem.at[turn, k])
+            foreign(near, i, chunks + i)
+
+        @pl.when((i == 2) & (tm == 0))
+        def _():
+            tail[...] = jnp.zeros_like(tail)
+
+        @pl.when((i == 2) & (tm == 1))
+        def _():
+            drain(rim, rim_sem.at[1])
+
+            def one(j, carry):
+                tail[2 * j] = rim[j, :8].astype(f32)
+                tail[2 * j + 1] = rim[j, 8:].astype(f32)
                 return carry
 
-            lax.fori_loop(0, 2, one, 0)
-
-        @pl.when((i == 2) & (tm == 0))
-        def _():
-            tail[...] = jnp.zeros_like(tail)
-
-        @pl.when((i == 2) & (tm == 1))
-        def _():
-            drain(rim, rim_sem.at[1])
-            tail[...] = rim[...]
+            lax.fori_loop(0, rim.shape[0], one, 0)
 
         @pl.when(i >= 1)
         def _():
@@ -666,7 +681,12 @@
 
         @pl.when((i == 1) & (tm == 0))
         def _():
-            tail_sent[...] = tail[...]
+            def one(j, carry):
+                pair_at = jnp.concatenate([tail[2 * j], tail[2 * j + 1]], axis=0)
+                tail_sent[j] = pair_at.astype(bf16)
+                return carry
+
+            lax.fori_loop(0, rim.shape[0], one, 0)
             pass_tail().start()
 
         return carry
@@ -689,9 +709,8 @@
 
     @pl.when(is_gate)
     def _():
-        def one(turn, carry):
-            for k in range(2):
-                wait_all(far_out.at[turn, k], far_sem.at[turn, k])
+        def one(slot, carry):
+            wait_all(far_out.at[slot], far_sem.at[slot])
             return carry
 
         lax.fori_loop(0, ring, one, 0)
@@ -719,7 +738,7 @@
     blocks = LANES // inner
     fold = LANES // (2 * chan)
     bf16, f32 = jnp.bfloat16, jnp.float32
-    ring = 2
+    ring = 4
 
     flat = filter_taps.reshape(-1)
     before, after = (inner - 1) * chan, halo * chan + LANES - flat.shape[0]
@@ -749,7 +768,7 @@
         scratch_shapes=[
             pltpu.VMEM((chunks, slots, pair, LANES), bf16),
             pltpu.VMEM((chunks, half, local, pair, LANES), bf16),
-            pltpu.VMEM((ring, 2, half, local, pair, LANES), bf16),
+            pltpu.VMEM((ring, half, local, pair, LANES), bf16),
             pltpu.VMEM((chunks, local, 2 * inputs, LANES), bf16),
             pltpu.VMEM((chunks, 2, local, 2 * inputs, LANES), bf16),
             pltpu.VMEM((2, local, 2 * inputs, LANES), bf16),
@@ -759,16 +778,17 @@
             pltpu.VMEM((group, bands * blocks, spans * 2 * chan), bf16),
             pltpu.VMEM((slots, pair, LANES), bf16),
             pltpu.VMEM((chan * pair, LANES), f32),
-            pltpu.VMEM((halo + LANES, LANES), f32),
+            pltpu.VMEM((group // fold, LANES, LANES), f32),
+            pltpu.VMEM((group, 8 + LANES // fold, LANES), f32),
             pltpu.VMEM((spans * 2 * chan, 2 * LANES), bf16),
-            pltpu.VMEM((bands * blocks * 2, LANES), f32),
+            pltpu.VMEM((2, bands * blocks * 2, LANES), f32),
             pltpu.VMEM((group, bands, 2 * blocks, LANES), bf16),
-            pltpu.VMEM((bands * group // fold, halo, LANES), f32),
-            pltpu.VMEM((bands * group // fold, halo, LANES), f32),
-            pltpu.VMEM((bands * group // fold, halo, LANES), f32),
+            pltpu.VMEM((bands * group, 8, LANES), f32),
+            pltpu.VMEM((bands * group // 2, 16, LANES), bf16),
+            pltpu.VMEM((bands * group // 2, 16, LANES), bf16),
             dma((chunks, n)),
             dma((chunks, half)),
-            dma((ring, 2, half)),
+            dma((ring, half)),
             dma((chunks,)),
             dma((chunks,)),
             dma((chunks, 2)),
@@ -802,6 +822,7 @@
 def on_device(voltages, pointing_table, beam_pointing, subband_order, live_subbands, filter_taps):
     local, _, inputs, local_time = voltages.shape
     beams = beam_pointing.shape[0]
+    tap_count, chan = filter_taps.shape
     n = lax.axis_size("sub")
     fits = (
         lax.axis_size("tm") == 2
@@ -811,6 +832,8 @@
         and local % 2 == 0
         and local_time % LANES == 0
         and local_time >= 4 * LANES
+        and chan * 8 == LANES
+        and tap_count <= chan + 1
     )
     plan = relay_plan if fits else direct_plan
     return plan(

time: 361 us -> 299 us (0.83)
  Pallas kernels: 344 us -> 281 us
    pallas_call x1, Pallas kernels: 344 us -> 281 us  [relay_plan(): pl.pallas_call(functools.partial(relay_kernel, n, chan), in_specs=[smem,...]
where the time goes in v2:
time: 299 us; the launch traced here: 298 us
  Pallas kernels  281 us (94%)
  local copies, waits for them, and re-layouts  16.7 us (6%)
    pallas_call x1, Pallas kernels, relay_plan(): pl.pallas_call(functools.partial(relay_kernel, n, chan), in_specs=[smem,...  281 us
    unnamed x1, local copies, waits for them, and re-layouts  11.4 us

profile of v2, /device:TPU:7, one launch (start us, length us, event | category | flops | bytes accessed | tf_op | source)
XLA Modules:
  0.0 298.5 jit_solution(14493722092863644795)
XLA Ops:
  0.7 0.8 reshape.123
  1.4 0.1 fusion.6
  1.5 0.1 fusion.20
  1.6 0.1 sine_convert_fusion
  1.7 0.1 copy.9
  1.8 1.0 fusion.21
  2.8 0.1 stack.110
  2.8 0.1 stack.108
  2.9 0.1 stack.107
  3.0 0.1 stack.106
  3.1 0.1 stack.105
  3.2 0.1 stack.104
  3.2 0.1 stack.103
  3.3 0.1 stack.102
  3.4 0.1 stack.109
  3.5 1.8 stack.118.taps_ref
  5.4 0.8 reshape.124.trig_ref
  6.1 281.0 %relay.1 = bf16[16,12,256,128]{3,2,1,0:T(8,128)(2,1)} custom-call(s32[192]{0:T(256)} %order_ref.1, s32[1]{0:T(128)S(6)} %copy.12.live_ref, s32[1,256]{1,0:T(1,128)} %bitcast.49, bf16[12,192,320]{2,1,0:T(8,128)(2,1)} %bitcast.48, f32[24,128]{1,0:T(8,128)} %stack.118.taps_ref, f32[32,256]{1,0:T(8,128)} %reshape.124.trig_ref, bf16[12,192,1024]{2,1,0:T(8,128)(2,1)} %bitcast.47), custom_call_target="tpu_custom_call" | custom-call | flops 20000000000 | bytes 20000000 | tf_op jit(solution)/shard_map/relay/pallas_call | solution.py:763
  287.1 11.4 %copy.13 = bf16[16,12,2,16384]{3,2,1,0:T(2,128)(2,1)} copy(bf16[16,12,2,16384]{3,2,1,0:T(2,128)(2,1)} %bitcast.46) | data formatting | bytes 25165824
  (4 shorter events, 0.0 us)

commit v3 on v2

--- a/solution.py
+++ b/solution.py
@@ -3,6 +3,7 @@
 
 import jax
 import jax.numpy as jnp
+import numpy as np
 from jax import lax
 from jax.experimental import pallas as pl
 from jax.experimental.pallas import tpu as pltpu
@@ -331,7 +332,7 @@
     lhs,
     stage,
     wide,
-    line,
+    select,
     steps,
     mat,
     made,
@@ -339,6 +340,10 @@
     tail,
     tail_sent,
     rim,
+    head,
+    joint,
+    redo,
+    mended,
     z_sem,
     own_sem,
     far_sem,
@@ -351,6 +356,7 @@
     fwd_recv,
     rim_sem,
     out_sem,
+    mend_sem,
 ):
     f32, bf16 = jnp.float32, jnp.bfloat16
     half, quarter = n // 2, n // 4
@@ -363,6 +369,10 @@
     halo = spans - inner
     blocks = LANES // inner
     ring = far_out.shape[0]
+    pitch = wide.shape[0] // chan
+    parts = volt_recv.shape[2]
+    batch = slots_here // parts
+    unroll = math.gcd(batch, 6)
 
     me, tm = lax.axis_index("sub"), lax.axis_index("tm")
     side, pos = lax.div(me, half), lax.rem(me, half)
@@ -389,21 +399,23 @@
         )
 
     def send_volts(c):
-        pltpu.make_async_remote_copy(
-            src_ref=volts.at[c],
-            dst_ref=far_volts.at[c, rank],
-            send_sem=volt_send.at[c],
-            recv_sem=volt_recv.at[c, rank],
-            device_id=(gate, tm),
-            device_id_type=MESH,
-        ).start()
-
-    def send_all(sent, src, c, sems):
+        for part in range(parts):
+            some = pl.ds(part * batch, batch)
+            pltpu.make_async_remote_copy(
+                src_ref=volts.at[c, some],
+                dst_ref=far_volts.at[c, rank, some],
+                send_sem=volt_send.at[c],
+                recv_sem=volt_recv.at[c, rank, part],
+                device_id=(gate, tm),
+                device_id_type=MESH,
+            ).start()
+
+    def send_all(sent, src, c, sems, first, count):
         def to(j, carry):
             there = lax.rem(pos + 1 + j, half)
             pltpu.make_async_remote_copy(
-                src_ref=sent.at[there],
-                dst_ref=z.at[c, pl.ds(src * slots_here, slots_here)],
+                src_ref=sent.at[there, pl.ds(first, count)],
+                dst_ref=z.at[c, pl.ds(src * slots_here + first, count)],
                 send_sem=sems.at[there],
                 recv_sem=z_sem.at[c, src],
                 device_id=(side * half + there, tm),
@@ -421,8 +433,9 @@
 
         lax.fori_loop(0, half - 1, one, 0)
 
-    def form(weights, signal, sent, src, c):
-        def one(s, carry):
+    def form(weights, signal, sent, src, c, first, count):
+        def one(j, carry):
+            s = first + j
             formed = jnp.dot(
                 weights[s][:, :inputs2], signal[s], preferred_element_type=f32
             ).astype(bf16)
@@ -430,13 +443,14 @@
                 sent[d, s] = formed[d * pair : (d + 1) * pair]
             return carry
 
-        lax.fori_loop(0, slots_here, one, 0, unroll=4)
-
-        def keep(s, carry):
+        lax.fori_loop(0, count, one, 0, unroll=unroll)
+
+    def keep(sent, src, c):
+        def one(s, carry):
             z[c, src * slots_here + s] = sent[pos, s]
             return carry
 
-        lax.fori_loop(0, slots_here, keep, 0)
+        lax.fori_loop(0, slots_here, one, 0, unroll=unroll)
 
     def prepare(picked, weights, at):
         w = picked.astype(f32)
@@ -449,8 +463,7 @@
             weights[at, d * pair : d * pair + group] = upper[rows]
             weights[at, d * pair + group : (d + 1) * pair] = lower[rows]
 
-    for step in range(chunks):
-        load(chunk_at(step)).start()
+    load(chunk_at(0)).start()
 
     def send_later(step, carry):
         load(chunk_at(step)).wait()
@@ -458,6 +471,8 @@
         return carry
 
     send_later(0, 0)
+    for step in range(1, chunks):
+        load(chunk_at(step)).start()
 
     pointings = table_ref.shape[2]
     hot = (
@@ -491,11 +506,33 @@
 
     lax.fori_loop(0, slots_here, prepare_own, 0)
 
+    tap_count = taps_ref.shape[0]
+    repeat = lax.broadcasted_iota(jnp.int32, (chan, LANES), 0) == lax.rem(
+        lax.broadcasted_iota(jnp.int32, (chan, LANES), 1), chan
+    )
+    taps = jnp.dot(
+        taps_ref[...],
+        repeat.astype(f32),
+        precision=lax.Precision.HIGHEST,
+        preferred_element_type=f32,
+    )
+    tap_at = lax.broadcasted_iota(jnp.int32, (tap_count, LANES), 0)
+    time_at = lax.div(lax.broadcasted_iota(jnp.int32, (tap_count, LANES), 1), chan)
     for v in range(spans):
-        taps = taps_ref[v : v + 1, :]
+        row = jnp.sum(
+            jnp.where(time_at - tap_at == v - halo, taps, 0.0), axis=0, keepdims=True
+        )
         mat[v * 2 * chan : (v + 1) * 2 * chan] = (
-            jnp.concatenate([taps, taps], axis=1) * trig_ref[...]
+            jnp.concatenate([row, row], axis=1) * trig_ref[...]
         ).astype(bf16)
+    select_row = lax.broadcasted_iota(jnp.int32, (LANES, LANES), 0)
+    phases = LANES // (2 * chan)
+    select_time = lax.rem(select_row, LANES // phases) * phases + lax.div(
+        select_row, LANES // phases
+    )
+    select[...] = (
+        lax.broadcasted_iota(jnp.int32, (LANES, LANES), 1) == select_time
+    ).astype(bf16)
     tail[...] = jnp.zeros_like(tail)
 
     def foreign_weights(k):
@@ -530,9 +567,17 @@
         def _():
             wait_all(far_out.at[slot], far_sem.at[slot])
 
-        drain(far_volts.at[c, k], volt_recv.at[c, k])
-        form(far_w.at[k], far_volts.at[c, k], far_out.at[slot], source_of(k), c)
-        send_all(far_out.at[slot], source_of(k), c, far_sem.at[slot])
+        src = source_of(k)
+
+        def one(part, carry):
+            first = part * batch
+            drain(far_volts.at[c, k, pl.ds(first, batch)], volt_recv.at[c, k, part])
+            form(far_w.at[k], far_volts.at[c, k], far_out.at[slot], src, c, first, batch)
+            send_all(far_out.at[slot], src, c, far_sem.at[slot], first, batch)
+            return carry
+
+        lax.fori_loop(0, parts, one, 0)
+        keep(far_out.at[slot], src, c)
 
     width = 2 * chan
     fold = LANES // width
@@ -551,22 +596,20 @@
         return swap(first, second, width) + swap(third, fourth, width)
 
     def synthesise(i):
-        c = chunk_at(lax.rem(i - 1, chunks))
-
-        @pl.when(i <= chunks)
-        def _():
-            def one(src, carry):
-                local = (src == me) | (
-                    is_gate & (lax.div(src, half) == other) & (lax.rem(src, quarter) == lane)
-                )
-
-                @pl.when(jnp.logical_not(local))
-                def _():
-                    drain(z.at[c, pl.ds(src * slots_here, slots_here)], z_sem.at[c, src])
-
-                return carry
-
-            lax.fori_loop(0, n, one, 0)
+        c = chunk_at(i - 1)
+
+        def one(src, carry):
+            local = (src == me) | (
+                is_gate & (lax.div(src, half) == other) & (lax.rem(src, quarter) == lane)
+            )
+
+            @pl.when(jnp.logical_not(local))
+            def _():
+                drain(z.at[c, pl.ds(src * slots_here, slots_here)], z_sem.at[c, src])
+
+            return carry
+
+        lax.fori_loop(0, n, one, 0)
 
         def copy(s, carry):
             stage[s] = z[c, s]
@@ -578,28 +621,31 @@
             for k in range(chan):
                 alive = g * chan + k < live_ref[0]
                 block = stage[order_ref[g * chan + k]].astype(f32)
-                wide[k * pair : (k + 1) * pair] = jnp.where(alive, block, 0.0)
+                wide[k * pitch : k * pitch + pair] = jnp.where(alive, block, 0.0)
 
             for q in range(group // fold):
                 rows = [
-                    wide[pl.ds(p * group + q * fold + b, chan, stride=pair), :]
+                    wide[pl.ds(p * group + q * fold + b, chan, stride=pitch), :]
                     for b in range(fold)
                     for p in range(2)
                 ]
-                line[q] = jnp.concatenate(rows, axis=0).T
-                split = [line[q, pl.ds(w, LANES // fold, stride=fold), :] for w in range(fold)]
+                turned = lax.dot_general(
+                    select[...],
+                    jnp.concatenate(rows, axis=0).astype(bf16),
+                    (((1,), (1,)), ((), ())),
+                    preferred_element_type=f32,
+                )
+                size = LANES // fold
+                split = [turned[w * size : (w + 1) * size] for w in range(fold)]
                 for b, block in enumerate(exchange(split)):
                     beam = q * fold + b
                     at = g * group + beam
                     steps[beam, :8] = tail[at]
                     steps[beam, 8:] = block
                     tail[at] = block[LANES // fold - 8 :]
+                    head[lax.min(i - 1, 1), at] = block[:8]
                     for e in range(spans // fold):
-                        lhs[
-                            beam,
-                            pl.ds(pl.multiple_of(g * blocks, blocks), blocks),
-                            e * LANES : (e + 1) * LANES,
-                        ] = steps[
+                        lhs[e, beam, pl.ds(pl.multiple_of(g * blocks, blocks), blocks)] = steps[
                             beam, pl.ds(8 - halo // fold + e, blocks, stride=inner // fold), :
                         ].astype(bf16)
             return carry
@@ -612,24 +658,67 @@
             out_sem,
         )
 
-        @pl.when(i > 2)
+        @pl.when(i > 1)
         def _():
             drain(ready, out_sem)
 
         def emit(b, carry):
-            out = jnp.dot(lhs[b], mat[...], preferred_element_type=f32)
             rows = bands * blocks
-            turn = lax.rem(b, 2)
-            made[turn, pl.ds(0, rows, stride=2), :] = out[:, :LANES]
-            made[turn, pl.ds(1, rows, stride=2), :] = out[:, LANES:]
+            terms = [
+                lhs[e, pl.ds(b * fold, fold)].reshape(fold * rows, LANES)
+                for e in range(spans // fold)
+            ]
+            out = jnp.dot(
+                jnp.concatenate(terms, axis=1), mat[...], preferred_element_type=f32
+            )
+            made[pl.ds(0, fold * rows, stride=2), :] = out[:, :LANES]
+            made[pl.ds(1, fold * rows, stride=2), :] = out[:, LANES:]
+            for j in range(fold):
+                for g in range(bands):
+                    at = (j * bands + g) * 2 * blocks
+                    ready[b * fold + j, g] = made[at : at + 2 * blocks].astype(bf16)
+            return carry
+
+        lax.fori_loop(0, group // fold, emit, 0)
+        out_copy.start()
+
+    def patch():
+        rows = halo // inner + 2
+        opening = bands * rows
+
+        def restack(b, carry):
             for g in range(bands):
-                ready[b, g] = made[turn, g * 2 * blocks : (g + 1) * 2 * blocks].astype(bf16)
-            return carry
-
-        @pl.when(i > 1)
-        def _():
-            lax.fori_loop(0, group, emit, 0, unroll=2)
-            out_copy.start()
+                at = g * group + b
+                joint[g, :8] = tail[at]
+                joint[g, 8:] = head[0, at]
+                for e in range(spans // fold):
+                    redo[e, b, g * rows : (g + 1) * rows] = joint[
+                        g, pl.ds(8 - halo // fold + e, rows, stride=inner // fold), :
+                    ]
+            return carry
+
+        lax.fori_loop(0, group, restack, 0)
+        terms = [
+            redo[e].reshape(group * opening, LANES).astype(bf16) for e in range(spans // fold)
+        ]
+        out = jnp.dot(jnp.concatenate(terms, axis=1), mat[...], preferred_element_type=f32)
+        made[pl.ds(0, group * opening, stride=2), :] = out[:, :LANES]
+        made[pl.ds(1, group * opening, stride=2), :] = out[:, LANES:]
+
+        def place(b, carry):
+            for g in range(bands):
+                at = pl.multiple_of(b * opening * 2 + g * rows * 2, rows * 2)
+                mended[b, g] = made[pl.ds(at, rows * 2)].astype(bf16)
+            return carry
+
+        lax.fori_loop(0, group, place, 0)
+        c = chunk_at(0)
+        start = pl.multiple_of(c * 2 * blocks, 2 * blocks)
+        copy = pltpu.make_async_copy(
+            mended, out_ref.at[:, :, pl.ds(start, rows * 2)], mend_sem
+        )
+        copy.start()
+        copy.wait()
 
     def pass_tail():
         return pltpu.make_async_remote_copy(
@@ -644,8 +733,9 @@
     def early(i, carry):
         c = chunk_at(i)
 
-        form(own_w, volts.at[c], own_out.at[c], me, c)
-        send_all(own_out.at[c], me, c, own_sem.at[c])
+        form(own_w, volts.at[c], own_out.at[c], me, c, 0, slots_here)
+        send_all(own_out.at[c], me, c, own_sem.at[c], 0, slots_here)
+        keep(own_out.at[c], me, c)
 
         @pl.when(is_gate)
         def _():
@@ -691,7 +781,8 @@
 
         return carry
 
-    lax.fori_loop(0, chunks + 2, step, 0)
+    lax.fori_loop(0, chunks + 1, step, 0)
+    patch()
 
     drain(ready, out_sem)
     drain(chosen.at[other, mine], w_send)
@@ -714,6 +805,21 @@
             return carry
 
         lax.fori_loop(0, ring, one, 0)
+
+
+def hand_over_kernel(in_ref, out_ref, held, in_sem, out_sem):
+    count = held.shape[0]
+    reads = [pltpu.make_async_copy(in_ref.at[b], held.at[b], in_sem.at[b]) for b in range(count)]
+    writes = [
+        pltpu.make_async_copy(held.at[b], out_ref.at[b], out_sem.at[b]) for b in range(count)
+    ]
+    for read in reads:
+        read.start()
+    for read, write in zip(reads, writes):
+        read.wait()
+        write.start()
+    for write in writes:
+        write.wait()
 
 
 def pair_of(chan):
@@ -740,18 +846,15 @@
     bf16, f32 = jnp.bfloat16, jnp.float32
     ring = 4
 
-    flat = filter_taps.reshape(-1)
-    before, after = (inner - 1) * chan, halo * chan + LANES - flat.shape[0]
-    flat = jnp.pad(flat, (before, after))
-    taps = jnp.stack(
-        [
-            flat[before + chan * (halo - v) : before + chan * (halo - v) + LANES]
-            for v in range(spans)
-        ]
-    )
-    trig = inverse_table(chan).astype(f32).transpose(2, 3, 0, 1)
-    trig = jnp.broadcast_to(trig[:, :, :, None, :], (2, chan, 2, inner, chan))
-    trig = trig.reshape(2 * chan, 2 * LANES)
+    at = np.arange(chan)
+    phase = (np.outer(at, at) % chan).astype(np.float32) * np.float32(2.0 * math.pi / chan)
+    cosine, sine = (
+        np.asarray(f(phase), jnp.bfloat16).astype(np.float32) for f in (np.cos, np.sin)
+    )
+    trig = np.stack([np.stack([cosine, -sine], 1), np.stack([sine, cosine], 1)])
+    trig = trig.transpose(2, 3, 0, 1)[:, :, :, None, :]
+    trig = np.broadcast_to(trig, (2, chan, 2, inner, chan))
+    trig = jnp.asarray(trig.reshape(2 * chan, 2 * LANES))
     signal = voltages.reshape(local, 2 * inputs, local_time)
     table = pointing_table.transpose(0, 1, 3, 2).reshape(local, 2 * inputs, pointings)
     lanes_in = 2 * LANES
@@ -775,28 +878,33 @@
             pltpu.VMEM((2, local, 2 * inputs, LANES), bf16),
             pltpu.VMEM((local, half * pair, lanes_in), bf16),
             pltpu.VMEM((2, local, half * pair, lanes_in), bf16),
-            pltpu.VMEM((group, bands * blocks, spans * 2 * chan), bf16),
+            pltpu.VMEM((spans // fold, group, bands * blocks, LANES), bf16),
             pltpu.VMEM((slots, pair, LANES), bf16),
-            pltpu.VMEM((chan * pair, LANES), f32),
-            pltpu.VMEM((group // fold, LANES, LANES), f32),
+            pltpu.VMEM((chan * (pair + 1), LANES), f32),
+            pltpu.VMEM((LANES, LANES), bf16),
             pltpu.VMEM((group, 8 + LANES // fold, LANES), f32),
             pltpu.VMEM((spans * 2 * chan, 2 * LANES), bf16),
-            pltpu.VMEM((2, bands * blocks * 2, LANES), f32),
+            pltpu.VMEM((fold * bands * blocks * 2, LANES), f32),
             pltpu.VMEM((group, bands, 2 * blocks, LANES), bf16),
             pltpu.VMEM((bands * group, 8, LANES), f32),
             pltpu.VMEM((bands * group // 2, 16, LANES), bf16),
             pltpu.VMEM((bands * group // 2, 16, LANES), bf16),
+            pltpu.VMEM((2, bands * group, 8, LANES), f32),
+            pltpu.VMEM((bands, 16, LANES), f32),
+            pltpu.VMEM((spans // fold, group, bands * (halo // inner + 2), LANES), f32),
+            pltpu.VMEM((group, bands, 2 * (halo // inner + 2), LANES), bf16),
             dma((chunks, n)),
             dma((chunks, half)),
             dma((ring, half)),
             dma((chunks,)),
             dma((chunks,)),
-            dma((chunks, 2)),
+            dma((chunks, 2, 1)),
             dma,
             dma((2,)),
             dma((2,)),
             dma((2,)),
             dma((2,)),
+            dma,
             dma,
         ],
         compiler_params=pltpu.CompilerParams(
@@ -811,10 +919,19 @@
         live_subbands,
         beam_pointing.reshape(1, beams),
         table,
-        taps,
+        filter_taps,
         trig,
         signal,
     )
+    out = pl.pallas_call(
+        hand_over_kernel,
+        in_specs=[anywhere],
+        out_specs=anywhere,
+        out_shape=jax.ShapeDtypeStruct(out.shape, bf16),
+        scratch_shapes=[pltpu.VMEM(out.shape, bf16), dma((group,)), dma((group,))],
+        compiler_params=pltpu.CompilerParams(vmem_limit_bytes=VMEM),
+        name="hand_over",
+    )(out)
     out = out.reshape(group, bands, blocks * chunks, 2, LANES).transpose(0, 1, 3, 2, 4)
     return out.reshape(group, bands, 2, local_time * chan)
 

time: 299 us -> 269 us (0.90)
  local copies, waits for them, and re-layouts: 16.7 us -> 0 us
  Pallas kernels: 281 us -> 268 us
    pallas_call x1, Pallas kernels: 281 us -> 259 us  [relay_plan(): pl.pallas_call(functools.partial(relay_kernel, n, chan), in_specs=[smem,...]
    unnamed x1 -> x0, local copies, waits for them, and re-layouts: 11.4 us -> none
    pallas_call x0 -> x1, Pallas kernels: none -> 9.03 us  [relay_plan(): pl.pallas_call(hand_over_kernel, in_specs=[anywhere], out_specs=anywhere,...]
where the time goes in v3:
time: 269 us
  Pallas kernels  268 us (100%)
    pallas_call x1, Pallas kernels, relay_plan(): pl.pallas_call(functools.partial(relay_kernel, n, chan), in_specs=[smem,...  259 us
    pallas_call x1, Pallas kernels, relay_plan(): pl.pallas_call(hand_over_kernel, in_specs=[anywhere], out_specs=anywhere,...  9.03 us

profile of v3, /device:TPU:7, one launch (start us, length us, event | category | flops | bytes accessed | tf_op | source)
XLA Modules:
  0.0 269.1 jit_solution(16026610257053105006)
XLA Ops:
  0.7 259.4 %relay.1.in_ref = bf16[16,12,256,128]{3,2,1,0:T(8,128)(2,1)} custom-call(s32[192]{0:T(256)} %order_ref.1, s32[1]{0:T(128)S(6)} %copy.9.live_ref, s32[1,256]{1,0:T(1,128)} %bitcast.12, bf16[12,192,320]{2,1,0:T(8,128)(2,1)} %bitcast.11, f32[16,16]{1,0:T(8,128)} %taps_ref.1, f32[32,256]{1,0:T(8,128)} %constant.2.clone.trig_ref, bf16[12,192,1024]{2,1,0:T(8,128)(2,1)} %bitcast.10), custom_call_target="tpu_custom_call" | custom-call | flops 20000000000 | bytes 20000000 | tf_op jit(solution)/shard_map/relay/pallas_call | solution.py:866
  260.1 9.0 %hand_over.1 = bf16[16,12,256,128]{3,2,1,0:T(8,128)(2,1)} custom-call(bf16[16,12,256,128]{3,2,1,0:T(8,128)(2,1)} %relay.1.in_ref), custom_call_target="tpu_custom_call" | custom-call | tf_op jit(solution)/shard_map/hand_over/pallas_call | solution.py:926

commit v4 on v3

--- a/solution.py
+++ b/solution.py
@@ -369,7 +369,8 @@
     halo = spans - inner
     blocks = LANES // inner
     ring = far_out.shape[0]
-    pitch = wide.shape[0] // chan
+    together = wide.shape[0]
+    pitch = wide.shape[1] // chan
     parts = volt_recv.shape[2]
     batch = slots_here // parts
     unroll = math.gcd(batch, 6)
@@ -617,15 +618,15 @@
 
         lax.fori_loop(0, stage.shape[0], copy, 0, unroll=4)
 
-        def gather(g, carry):
+        def gather(g, at_once):
             for k in range(chan):
                 alive = g * chan + k < live_ref[0]
                 block = stage[order_ref[g * chan + k]].astype(f32)
-                wide[k * pitch : k * pitch + pair] = jnp.where(alive, block, 0.0)
+                wide[at_once, k * pitch : k * pitch + pair] = jnp.where(alive, block, 0.0)
 
             for q in range(group // fold):
                 rows = [
-                    wide[pl.ds(p * group + q * fold + b, chan, stride=pitch), :]
+                    wide[at_once, pl.ds(p * group + q * fold + b, chan, stride=pitch), :]
                     for b in range(fold)
                     for p in range(2)
                 ]
@@ -640,17 +641,21 @@
                 for b, block in enumerate(exchange(split)):
                     beam = q * fold + b
                     at = g * group + beam
-                    steps[beam, :8] = tail[at]
-                    steps[beam, 8:] = block
+                    steps[at_once, beam, :8] = tail[at]
+                    steps[at_once, beam, 8:] = block
                     tail[at] = block[LANES // fold - 8 :]
                     head[lax.min(i - 1, 1), at] = block[:8]
                     for e in range(spans // fold):
                         lhs[e, beam, pl.ds(pl.multiple_of(g * blocks, blocks), blocks)] = steps[
-                            beam, pl.ds(8 - halo // fold + e, blocks, stride=inner // fold), :
+                            at_once, beam, pl.ds(8 - halo // fold + e, blocks, stride=inner // fold), :
                         ].astype(bf16)
-            return carry
-
-        lax.fori_loop(0, bands, gather, 0)
+
+        def several(j, carry):
+            for at_once in range(together):
+                gather(j * together + at_once, at_once)
+            return carry
+
+        lax.fori_loop(0, bands // together, several, 0)
 
         out_copy = pltpu.make_async_copy(
             ready,
@@ -730,12 +735,22 @@
             device_id_type=MESH,
         )
 
-    def early(i, carry):
+    def own(i, carry):
         c = chunk_at(i)
-
         form(own_w, volts.at[c], own_out.at[c], me, c, 0, slots_here)
         send_all(own_out.at[c], me, c, own_sem.at[c], 0, slots_here)
         keep(own_out.at[c], me, c)
+        return carry
+
+    ahead, prompt = 3, chunks
+    lax.fori_loop(0, ahead, own, 0)
+
+    def early(i, carry):
+        later = i + ahead
+
+        @pl.when((later < prompt) | (jnp.logical_not(is_gate) & (later < chunks)))
+        def _():
+            own(later, 0)
 
         @pl.when(is_gate)
         def _():
@@ -749,6 +764,10 @@
         @pl.when(is_gate & (i < chunks))
         def _():
             foreign(near, i, chunks + i)
+
+        @pl.when(is_gate & (i + prompt < chunks))
+        def _():
+            own(i + prompt, 0)
 
         @pl.when((i == 2) & (tm == 0))
         def _():
@@ -845,6 +864,7 @@
     fold = LANES // (2 * chan)
     bf16, f32 = jnp.bfloat16, jnp.float32
     ring = 4
+    together = math.gcd(bands, 2)
 
     at = np.arange(chan)
     phase = (np.outer(at, at) % chan).astype(np.float32) * np.float32(2.0 * math.pi / chan)
@@ -880,9 +900,9 @@
             pltpu.VMEM((2, local, half * pair, lanes_in), bf16),
             pltpu.VMEM((spans // fold, group, bands * blocks, LANES), bf16),
             pltpu.VMEM((slots, pair, LANES), bf16),
-            pltpu.VMEM((chan * (pair + 1), LANES), f32),
+            pltpu.VMEM((together, chan * (pair + 1), LANES), f32),
             pltpu.VMEM((LANES, LANES), bf16),
-            pltpu.VMEM((group, 8 + LANES // fold, LANES), f32),
+            pltpu.VMEM((together, group, 8 + LANES // fold, LANES), f32),
             pltpu.VMEM((spans * 2 * chan, 2 * LANES), bf16),
             pltpu.VMEM((fold * bands * blocks * 2, LANES), f32),
             pltpu.VMEM((group, bands, 2 * blocks, LANES), bf16),
@@ -898,7 +918,7 @@
             dma((ring, half)),
             dma((chunks,)),
             dma((chunks,)),
-            dma((chunks, 2, 1)),
+            dma((chunks, 2, 2)),
             dma,
             dma((2,)),
             dma((2,)),

time: 269 us -> 255 us (0.948)
  Pallas kernels: 268 us -> 253 us
    pallas_call x1, Pallas kernels: 259 us -> 244 us  [relay_plan(): pl.pallas_call(functools.partial(relay_kernel, n, chan), in_specs=[smem,...]
where the time goes in v4:
time: 255 us; the launch traced here: 254 us
  Pallas kernels  253 us (99%)
    pallas_call x1, Pallas kernels, relay_plan(): pl.pallas_call(functools.partial(relay_kernel, n, chan), in_specs=[smem,...  244 us
    pallas_call x1, Pallas kernels, relay_plan(): pl.pallas_call(hand_over_kernel, in_specs=[anywhere], out_specs=anywhere,...  9.03 us

profile of v4, /device:TPU:7, one launch (start us, length us, event | category | flops | bytes accessed | tf_op | source)
XLA Modules:
  0.0 253.9 jit_solution(175282921675728680)
XLA Ops:
  0.7 244.2 %relay.1.in_ref = bf16[16,12,256,128]{3,2,1,0:T(8,128)(2,1)} custom-call(s32[192]{0:T(256)} %order_ref.1, s32[1]{0:T(128)S(6)} %copy.9.live_ref, s32[1,256]{1,0:T(1,128)} %bitcast.12, bf16[12,192,320]{2,1,0:T(8,128)(2,1)} %bitcast.11, f32[16,16]{1,0:T(8,128)} %taps_ref.1, f32[32,256]{1,0:T(8,128)} %constant.2.clone.trig_ref, bf16[12,192,1024]{2,1,0:T(8,128)(2,1)} %bitcast.10), custom_call_target="tpu_custom_call" | custom-call | flops 20000000000 | bytes 20000000 | tf_op jit(solution)/shard_map/relay/pallas_call | solution.py:886
  244.9 9.0 %hand_over.1 = bf16[16,12,256,128]{3,2,1,0:T(8,128)(2,1)} custom-call(bf16[16,12,256,128]{3,2,1,0:T(8,128)(2,1)} %relay.1.in_ref), custom_call_target="tpu_custom_call" | custom-call | tf_op jit(solution)/shard_map/hand_over/pallas_call | solution.py:946

commit v5 on v4

--- a/solution.py
+++ b/solution.py
@@ -864,7 +864,7 @@
     fold = LANES // (2 * chan)
     bf16, f32 = jnp.bfloat16, jnp.float32
     ring = 4
-    together = math.gcd(bands, 2)
+    together = math.gcd(bands, 4)
 
     at = np.arange(chan)
     phase = (np.outer(at, at) % chan).astype(np.float32) * np.float32(2.0 * math.pi / chan)

time: 255 us -> 255 us (level)
  no operation moved by 1% of the time
where the time goes in v5:
time: 255 us; the launch traced here: 254 us
  Pallas kernels  253 us (99%)
    pallas_call x1, Pallas kernels, relay_plan(): pl.pallas_call(functools.partial(relay_kernel, n, chan), in_specs=[smem,...  244 us
    pallas_call x1, Pallas kernels, relay_plan(): pl.pallas_call(hand_over_kernel, in_specs=[anywhere], out_specs=anywhere,...  9.03 us

profile of v5, /device:TPU:7, one launch (start us, length us, event | category | flops | bytes accessed | tf_op | source)
XLA Modules:
  0.0 253.5 jit_solution(1903475603571931327)
XLA Ops:
  0.7 243.8 %relay.1.in_ref = bf16[16,12,256,128]{3,2,1,0:T(8,128)(2,1)} custom-call(s32[192]{0:T(256)} %order_ref.1, s32[1]{0:T(128)S(6)} %copy.9.live_ref, s32[1,256]{1,0:T(1,128)} %bitcast.12, bf16[12,192,320]{2,1,0:T(8,128)(2,1)} %bitcast.11, f32[16,16]{1,0:T(8,128)} %taps_ref.1, f32[32,256]{1,0:T(8,128)} %constant.2.clone.trig_ref, bf16[12,192,1024]{2,1,0:T(8,128)(2,1)} %bitcast.10), custom_call_target="tpu_custom_call" | custom-call | flops 20000000000 | bytes 20000000 | tf_op jit(solution)/shard_map/relay/pallas_call | solution.py:886
  244.5 9.0 %hand_over.1 = bf16[16,12,256,128]{3,2,1,0:T(8,128)(2,1)} custom-call(bf16[16,12,256,128]{3,2,1,0:T(8,128)(2,1)} %relay.1.in_ref), custom_call_target="tpu_custom_call" | custom-call | tf_op jit(solution)/shard_map/hand_over/pallas_call | solution.py:946
